TPU v7x, 32 devices: a whole 2x2x4 slice. The times are simulated.
32 devices in a mesh: dap: 32 (over z, y, x, core), ch: 1.
Axes of the slice: x: 2, y: 2, z: 4, core: 2. Of those that a mesh axis runs over, the one named last changes fastest.
Arguments:
- alignment_embedding: bfloat16 [128, 128, 256], P(None, 'dap'), may hold values from -6 to 6
- couple_embedding: bfloat16 [128, 128, 128], P('dap', 'ch'), may hold values from -6 to 6
- tensor_first_matrix: bfloat16 [256, 32], P(None, 'ch'), may hold values from -0.375 to 0.375
- tensor_second_matrix: bfloat16 [256, 32], replicated, may hold values from -0.375 to 0.375
- tensor_final_matrix: bfloat16 [1024, 128], P('ch'), may hold values from -1 to 1
- trimul_entry_matrix: bfloat16 [4, 128, 128], replicated, may hold values from -0.5 to 0.5
- trimul_sigmoid_matrix: bfloat16 [128, 128], replicated, may hold values from -0.5 to 0.5
- trimul_final_matrix: bfloat16 [128, 128], replicated, may hold values from -0.5 to 0.5
Outputs:
- pair_out: bfloat16 [128, 128, 128], P('dap', 'ch')
All inputs are finite; a program needn't handle non-finite values.
Results may differ from a plain program's by a relative error of at most 0.014.
Values may be sent and summed in bfloat16 or wider, within the bound.
A program may use at most 64 MiB of HBM per device.

v0:
```python
import jax
import jax.numpy as jnp
from jax import lax
from jax.sharding import PartitionSpec as P


def standardize_fn(value, axis):
    mean = jnp.mean(value, axis=axis, keepdims=True)
    centred = value - mean
    var = jnp.mean(centred * centred, axis=axis, keepdims=True)
    return centred * lax.rsqrt(var + 1e-05)


def outer_update(first_operand, right_rows, w_out, alignment_height):
    rows = first_operand.shape[1]
    outer = jnp.einsum(
        "sic,sje->ijce", first_operand, right_rows, preferred_element_type=jnp.float32
    )
    outer = (outer * (1.0 / alignment_height)).astype(jnp.bfloat16)
    outer = outer.reshape(rows, right_rows.shape[1], first_operand.shape[2] * right_rows.shape[2])
    return jnp.einsum("ijf,fz->ijz", outer, w_out, preferred_element_type=jnp.float32)


def per_device(
    alignment_embedding,
    couple_embedding,
    tensor_first_matrix,
    tensor_second_matrix,
    tensor_final_matrix,
    trimul_entry_matrix,
    trimul_sigmoid_matrix,
    trimul_final_matrix,
):
    alignment_height = alignment_embedding.shape[0]
    columns = couple_embedding.shape[1]
    alignment_standardized = standardize_fn(alignment_embedding.astype(jnp.float32), -1).astype(
        jnp.bfloat16
    )
    second_operand = jnp.einsum(
        "ziv,vl->zil",
        alignment_standardized,
        tensor_second_matrix,
        preferred_element_type=jnp.float32,
    ).astype(jnp.bfloat16)
    right_all = lax.all_gather(second_operand, "dap", axis=1, tiled=True)
    first_operand = jnp.einsum(
        "ziv,vl->zil",
        alignment_standardized,
        tensor_first_matrix,
        preferred_element_type=jnp.float32,
    ).astype(jnp.bfloat16)
    terms = outer_update(first_operand, right_all, tensor_final_matrix, alignment_height)
    totals = lax.psum(terms.astype(jnp.bfloat16), "ch").astype(jnp.float32)
    update = lax.dynamic_slice_in_dim(totals, lax.axis_index("ch") * columns, columns, 1)
    lifted = (couple_embedding.astype(jnp.float32) + update).astype(jnp.bfloat16)
    normed = standardize_fn(lifted.astype(jnp.float32), -1).astype(jnp.bfloat16)
    projected = jnp.einsum(
        "rkz,qzc->qcrk", normed, trimul_entry_matrix, preferred_element_type=jnp.float32
    )
    left_t = (jax.nn.sigmoid(projected[0]) * projected[1]).astype(jnp.bfloat16)
    right_t = (jax.nn.sigmoid(projected[2]) * projected[3]).astype(jnp.bfloat16)
    left_cols, right_cols = (
        lax.all_to_all(left_t, "dap", split_axis=0, concat_axis=1, tiled=True),
        lax.all_to_all(right_t, "dap", split_axis=0, concat_axis=1, tiled=True),
    )
    product = jnp.einsum("cik,cjk->cij", left_cols, right_cols, preferred_element_type=jnp.float32)
    returned = lax.all_to_all(
        product.astype(jnp.bfloat16), "dap", split_axis=1, concat_axis=0, tiled=True
    ).astype(product.dtype)
    summed = lax.psum_scatter(returned.astype(jnp.bfloat16), "ch", scatter_dimension=2, tiled=True)
    tri_n = standardize_fn(summed.astype(jnp.float32), 0).astype(jnp.bfloat16)
    out = jnp.einsum("crj,cz->rjz", tri_n, trimul_final_matrix, preferred_element_type=jnp.float32)
    gate = jax.nn.sigmoid(
        jnp.einsum("rjz,zy->rjy", normed, trimul_sigmoid_matrix, preferred_element_type=jnp.float32)
    )
    return (lifted.astype(jnp.float32) + gate * out).astype(jnp.bfloat16)


def solution(mesh):
    placed = (
        P(None, "dap", None),
        P("dap", "ch", None),
        P(None, "ch"),
        P(),
        P("ch", None),
        P(),
        P(),
        P(),
    )
    return jax.shard_map(
        per_device, mesh=mesh, in_specs=placed, out_specs=P("dap", "ch", None), check_vma=False
    )
```

profile of v0, /device:TPU:0, one launch (start us, length us, event | category | flops | bytes accessed | tf_op | source)
XLA Modules:
  0.0 114.2 jit_solution(17043596067753059552)
XLA Ops:
  6.5 0.0 copy-start
  6.5 0.0 copy-start.1
  6.5 0.0 copy-start.7
  6.5 0.0 copy-start.2
  6.5 0.0 all-gather.2.cloned.1.call-start
  6.6 1.2 %convert_reduce_fusion = f32[128,4]{1,0:T(8,128)S(1)} fusion(bf16[128,4,256]{2,1,0:T(4,128)(2,1)} %param.8), kind=kLoop, calls=%fused_computation.21 | loop fusion | flops 261632 | bytes 264192 | tf_op jit(solution)/shard_map/reduce_sum | solution.py:8
  7.8 0.0 copy-start.5
  7.8 1.3 %fusion.14 = f32[128,4]{1,0:T(8,128)S(1)} fusion(bf16[128,4,256]{2,1,0:T(4,128)(2,1)} %param.8, f32[128,4]{1,0:T(8,128)S(1)} %broadcast_multiply_fusion), kind=kLoop, calls=%fused_computation.24 | loop fusion | flops 523776 | bytes 266240 | tf_op jit(solution)/shard_map/reduce_sum | solution.py:10
  9.2 0.0 copy-done.1
  9.2 0.3 fusion.15
  9.6 0.0 copy-done.7
  9.6 0.8 convolution_convert_fusion.3
  10.4 0.0 all-gather.2.cloned.1.call-update
  10.4 0.0 copy-done.2
  10.4 0.1 copy.34
  10.5 56.3 %all-gather.2.cloned.1.call-done = bf16[128,128,32]{0,2,1:T(8,128)(2,1)} async-done(((bf16[128,4,32]{0,2,1:T(8,128)(2,1)}), bf16[128,128,32]{0,2,1:T(8,128)(2,1)}) %all-gather.2.cloned.1.call-update) | async-done | bytes 1048592 | tf_op jit(solution)/shard_map/all_gather | solution.py:45
  66.9 0.0 copy-done.5
  66.9 1.9 %fusion = bf16[4,128,32,32]{1,2,0,3:T(8,128)(2,1)S(1)} fusion(bf16[128,128,32,1]{0,2,1,3:T(8,128)(2,1)} %bitcast.65, bf16[128,4,256]{2,1,0:T(4,128)(2,1)S(1)} %fusion.15, bf16[256,32]{0,1:T(8,128)(2,1)S(1)} %copy-done.5), kind=kOutput, calls=%fused_computation.1 | convolution fusion | flops 143671296 | bytes 2375680 | tf_op jit(solution)/shard_map/sic,sje->ijce/dot_general | solution.py:16
  68.8 0.7 copy.38
  69.5 0.0 copy-start.3
  69.5 0.0 copy-done
  69.5 0.4 fusion.41
  69.9 0.5 copy-done.3
  70.4 0.3 convolution_bitcast_fusion
  70.7 0.1 fusion.35
  70.9 0.8 copy.47
  71.6 3.6 %all-to-all-start.1 = ((bf16[128,4,128]{2,1,0:T(4,128)(2,1)}), bf16[128,4,128]{2,1,0:T(4,128)(2,1)S(1)}, u32[]{:S(2)}, u32[]{:S(2)}) async-start(bf16[128,4,128]{2,1,0:T(4,128)(2,1)} %copy.47), calls=%async_computation.1 | async-start | bytes 262144 | tf_op jit(solution)/shard_map/all_to_all | solution.py:64
  75.2 0.8 copy.44
  76.0 7.4 %all-to-all-done.1 = bf16[128,4,128]{2,1,0:T(4,128)(2,1)S(1)} async-done(((bf16[128,4,128]{2,1,0:T(4,128)(2,1)}), bf16[128,4,128]{2,1,0:T(4,128)(2,1)S(1)}, u32[]{:S(2)}, u32[]{:S(2)}) %all-to-all-start.1) | async-done | bytes 131104 | tf_op jit(solution)/shard_map/all_to_all | solution.py:64
  83.4 2.6 %all-to-all-start = ((bf16[128,4,128]{2,1,0:T(4,128)(2,1)}), bf16[128,4,128]{2,1,0:T(4,128)(2,1)S(1)}, u32[]{:S(2)}, u32[]{:S(2)}) async-start(bf16[128,4,128]{2,1,0:T(4,128)(2,1)} %copy.44), calls=%async_computation | async-start | bytes 262144 | tf_op jit(solution)/shard_map/all_to_all | solution.py:63
  86.0 0.0 copy-start.6
  86.1 0.1 copy.49
  86.2 8.1 %all-to-all-done = bf16[128,4,128]{2,1,0:T(4,128)(2,1)S(1)} async-done(((bf16[128,4,128]{2,1,0:T(4,128)(2,1)}), bf16[128,4,128]{2,1,0:T(4,128)(2,1)S(1)}, u32[]{:S(2)}, u32[]{:S(2)}) %all-to-all-start) | async-done | bytes 131104 | tf_op jit(solution)/shard_map/all_to_all | solution.py:63
  94.2 0.1 copy.46
  94.3 0.2 convolution_convert_fusion
  94.6 0.8 copy.50
  95.3 2.6 %all-to-all-start.2 = ((bf16[4,128,128]{2,0,1:T(4,128)(2,1)}), bf16[4,128,128]{2,0,1:T(4,128)(2,1)S(1)}, u32[]{:S(2)}, u32[]{:S(2)}) async-start(bf16[4,128,128]{2,0,1:T(4,128)(2,1)} %copy.50), calls=%async_computation.2 | async-start | bytes 262144 | tf_op jit(solution)/shard_map/all_to_all | solution.py:67
  97.9 0.0 copy-done.6
  97.9 0.0 copy-start.4
  97.9 0.3 fusion.4
  98.2 7.9 %all-to-all-done.2 = bf16[4,128,128]{2,0,1:T(4,128)(2,1)S(1)} async-done(((bf16[4,128,128]{2,0,1:T(4,128)(2,1)}), bf16[4,128,128]{2,0,1:T(4,128)(2,1)S(1)}, u32[]{:S(2)}, u32[]{:S(2)}) %all-to-all-start.2) | async-done | bytes 131104 | tf_op jit(solution)/shard_map/all_to_all | solution.py:67
  106.1 0.1 bitcast_reduce_fusion
  106.2 0.1 fusion.25
  106.3 0.0 copy-done.4
  106.4 0.2 fusion.5
  106.6 0.8 copy.54
  (11 shorter events, 0.2 us)
Async XLA Ops:
  6.5 63.0 %copy-start = (bf16[1024,128]{1,0:T(8,128)(2,1)S(1)}, bf16[1024,128]{1,0:T(8,128)(2,1)}, u32[]{:S(2)}) copy-start(bf16[1024,128]{1,0:T(8,128)(2,1)} %param.12) | copy-start | bytes 786436
  6.5 2.7 %copy-start.1 = (bf16[128,4,256]{2,1,0:T(4,128)(2,1)S(1)}, bf16[128,4,256]{2,1,0:T(4,128)(2,1)}, u32[]{:S(2)}) copy-start(bf16[128,4,256]{2,1,0:T(4,128)(2,1)} %param.8) | copy-start | bytes 786436
  6.5 3.0 %copy-start.7 = (bf16[256,32]{0,1:T(8,128)(2,1)S(1)}, bf16[256,32]{0,1:T(8,128)(2,1)}, u32[]{:S(2)}) copy-start(bf16[256,32]{0,1:T(8,128)(2,1)} %param.11) | copy-start | bytes 49156
  6.5 3.9 %copy-start.2 = (bf16[4,128,128]{2,1,0:T(8,128)(2,1)S(1)}, bf16[4,128,128]{2,1,0:T(8,128)(2,1)}, u32[]{:S(2)}) copy-start(bf16[4,128,128]{2,1,0:T(8,128)(2,1)} %param.9) | copy-start | bytes 393220
  6.5 60.3 %all-gather.2.cloned.1.call-start = ((), (), s32[]{:S(2)}) async-start(), calls=%async_computation.3 | async-start | bytes 1081344 | tf_op jit(solution)/shard_map/all_gather | solution.py:45
  7.8 59.1 %copy-start.5 = (bf16[256,32]{0,1:T(8,128)(2,1)S(1)}, bf16[256,32]{0,1:T(8,128)(2,1)}, u32[]{:S(2)}) copy-start(bf16[256,32]{0,1:T(8,128)(2,1)} %param.10) | copy-start | bytes 49156
  69.5 0.9 copy-start.3
  71.6 11.8 %all-to-all-start.1 = ((bf16[128,4,128]{2,1,0:T(4,128)(2,1)}), bf16[128,4,128]{2,1,0:T(4,128)(2,1)S(1)}, u32[]{:S(2)}, u32[]{:S(2)}) async-start(bf16[128,4,128]{2,1,0:T(4,128)(2,1)} %copy.47), calls=%async_computation.1 | async-start | bytes 262144 | tf_op jit(solution)/shard_map/all_to_all | solution.py:64
  83.4 10.8 %all-to-all-start = ((bf16[128,4,128]{2,1,0:T(4,128)(2,1)}), bf16[128,4,128]{2,1,0:T(4,128)(2,1)S(1)}, u32[]{:S(2)}, u32[]{:S(2)}) async-start(bf16[128,4,128]{2,1,0:T(4,128)(2,1)} %copy.44), calls=%async_computation | async-start | bytes 262144 | tf_op jit(solution)/shard_map/all_to_all | solution.py:63
  86.0 11.9 %copy-start.6 = (bf16[128,128]{1,0:T(8,128)(2,1)S(1)}, bf16[128,128]{1,0:T(8,128)(2,1)}, u32[]{:S(2)}) copy-start(bf16[128,128]{1,0:T(8,128)(2,1)} %param.14) | copy-start | bytes 98308
  95.3 10.8 %all-to-all-start.2 = ((bf16[4,128,128]{2,0,1:T(4,128)(2,1)}), bf16[4,128,128]{2,0,1:T(4,128)(2,1)S(1)}, u32[]{:S(2)}, u32[]{:S(2)}) async-start(bf16[4,128,128]{2,0,1:T(4,128)(2,1)} %copy.50), calls=%async_computation.2 | async-start | bytes 262144 | tf_op jit(solution)/shard_map/all_to_all | solution.py:67
  97.9 8.4 %copy-start.4 = (bf16[128,128]{1,0:T(8,128)(2,1)S(1)}, bf16[128,128]{1,0:T(8,128)(2,1)}, u32[]{:S(2)}) copy-start(bf16[128,128]{1,0:T(8,128)(2,1)} %param.15) | copy-start | bytes 98308
Sparse Core Ops, SparseCore 0:
  10.5 56.3 all-gather.1
where the time goes:
time: 115 us; the launch traced here: 114 us
  waiting for transfers between devices  79.7 us (69%)
  between operations  13.7 us (12%)
  starting transfers between devices  8.77 us (8%)
  local copies, waits for them, and re-layouts  4.68 us (4%)
  matrix products  4.1 us (4%)
  other arithmetic  3.28 us (3%)
    all_gather x1, waiting for transfers between devices, per_device(): right_all = lax.all_gather(second_operand, 'dap', axis=1, tiled=True)  56.3 us
    all_to_all x1, waiting for transfers between devices, per_device(): lax.all_to_all(left_t, 'dap', split_axis=0, concat_axis=1, tiled=True)  8.05 us
    all_to_all x1, waiting for transfers between devices, per_device(): lax.all_to_all(product.astype(jnp.bfloat16), 'dap', split_axis=1, concat_...  7.91 us
    all_to_all x1, waiting for transfers between devices, per_device(): lax.all_to_all(right_t, 'dap', split_axis=0, concat_axis=1, tiled=True)  7.41 us
    all_to_all x1, starting transfers between devices, per_device(): lax.all_to_all(right_t, 'dap', split_axis=0, concat_axis=1, tiled=True)  3.58 us
    all_to_all x1, starting transfers between devices, per_device(): lax.all_to_all(left_t, 'dap', split_axis=0, concat_axis=1, tiled=True)  2.58 us
    all_to_all x1, starting transfers between devices, per_device(): lax.all_to_all(product.astype(jnp.bfloat16), 'dap', split_axis=1, concat_...  2.58 us
  transfers between devices with their start and end apart: 4, of which 4 were waited for; matrix products, arithmetic and copies ran while one was open for 1% of the time, Pallas kernels for 0%

commit v1 on v0

--- a/solution.py
+++ b/solution.py
@@ -1,7 +1,14 @@
+import functools
+
 import jax
 import jax.numpy as jnp
 from jax import lax
+from jax.experimental import pallas as pl
+from jax.experimental.pallas import tpu as pltpu
 from jax.sharding import PartitionSpec as P
+
+CORES = 2
+PLANE = 4
 
 
 def standardize_fn(value, axis):
@@ -76,7 +83,211 @@
     return (lifted.astype(jnp.float32) + gate * out).astype(jnp.bfloat16)
 
 
+def remote(src, dst, send_sem, recv_sem, peer):
+    return pltpu.make_async_remote_copy(
+        src_ref=src,
+        dst_ref=dst,
+        send_sem=send_sem,
+        recv_sem=recv_sem,
+        device_id={"dap": peer},
+        device_id_type=pl.DeviceIdType.MESH,
+    )
+
+
+def signal(peer):
+    pl.semaphore_signal(
+        pltpu.get_barrier_semaphore(),
+        inc=1,
+        device_id={"dap": peer},
+        device_id_type=pl.DeviceIdType.MESH,
+    )
+
+
+def gather_kernel(n, block, out, zs, zr, ps, pr, cs, cr):
+    depth = n // (CORES * PLANE)
+    me = lax.axis_index("dap")
+    core, p, z = me % CORES, (me // CORES) % PLANE, me // (CORES * PLANE)
+
+    def device(z_, p_, core_):
+        return (z_ * PLANE + p_) * CORES + core_
+
+    def source(zi, q):
+        return device((z - zi + depth) % depth, (p - q + PLANE) % PLANE, core)
+
+    partner = me + 1 - 2 * core
+    for zi in range(1, depth):
+        signal(device((z + zi) % depth, p, core))
+    for q in range(1, PLANE):
+        signal(device(z, (p + q) % PLANE, core))
+    signal(partner)
+    pl.semaphore_wait(pltpu.get_barrier_semaphore(), depth + PLANE - 1)
+
+    copies = []
+
+    def send(src, slot, send_sem, recv_sem, peer):
+        copy = remote(src, out.at[slot], send_sem, recv_sem, peer)
+        copy.start()
+        copies.append(copy)
+        return copy
+
+    along = {}
+    for zi in range(1, depth):
+        along[zi] = send(block, me, zs.at[zi], zr.at[zi], device((z + zi) % depth, p, core))
+    out[me] = block[...]
+    across = {}
+    for zi in range(depth):
+        slot = source(zi, 0)
+        if zi:
+            along[zi].wait_recv()
+        src = out.at[slot] if zi else block
+        for q in range(1, PLANE):
+            across[zi, q] = send(
+                src, slot, ps.at[zi, q], pr.at[zi, q], device(z, (p + q) % PLANE, core)
+            )
+        across[zi, 0] = send(src, slot, cs.at[zi, 0], cr.at[zi, 0], partner)
+    over = [across[zi, 0] for zi in range(depth)]
+    for zi in range(depth):
+        for q in range(1, PLANE):
+            across[zi, q].wait_recv()
+            slot = source(zi, q)
+            over.append(send(out.at[slot], slot, cs.at[zi, q], cr.at[zi, q], partner))
+    for copy in over:
+        copy.wait_recv()
+    for copy in copies:
+        copy.wait_send()
+
+
+def gather(block, n):
+    depth = n // (CORES * PLANE)
+    return pl.pallas_call(
+        functools.partial(gather_kernel, n),
+        out_shape=jax.ShapeDtypeStruct((n,) + block.shape, block.dtype),
+        in_specs=[pl.BlockSpec(memory_space=pltpu.VMEM)],
+        out_specs=pl.BlockSpec(memory_space=pltpu.VMEM),
+        scratch_shapes=[
+            pltpu.SemaphoreType.DMA((depth,)),
+            pltpu.SemaphoreType.DMA((depth,)),
+            pltpu.SemaphoreType.DMA((depth, PLANE)),
+            pltpu.SemaphoreType.DMA((depth, PLANE)),
+            pltpu.SemaphoreType.DMA((depth, PLANE)),
+            pltpu.SemaphoreType.DMA((depth, PLANE)),
+        ],
+        compiler_params=pltpu.CompilerParams(collective_id=0, has_side_effects=True),
+    )(block)
+
+
+def triangle_kernel(n, left, right, out, lrecv, rrecv, back, ls, lr, rs, rr, bs, br):
+    me = lax.axis_index("dap")
+    per, rows, width = left.shape[1:]
+
+    def greet(d, carry):
+        signal((me + d) % n)
+        return carry
+
+    lax.fori_loop(1, n, greet, 0)
+    pl.semaphore_wait(pltpu.get_barrier_semaphore(), n - 1)
+
+    def there(d):
+        peer = (me + d) % n
+        return (
+            remote(left.at[peer], lrecv.at[me], ls.at[d], lr.at[d], peer),
+            remote(right.at[peer], rrecv.at[me], rs.at[d], rr.at[d], peer),
+        )
+
+    def home(d):
+        peer = (me + d) % n
+        return (remote(back.at[peer], out.at[me], bs.at[d], br.at[d], peer),)
+
+    def run(make, action):
+        def step(d, carry):
+            for copy in make(d):
+                getattr(copy, action)()
+            return carry
+
+        lax.fori_loop(1, n, step, 0)
+
+    run(there, "start")
+    lrecv[me] = left[me]
+    rrecv[me] = right[me]
+    run(there, "wait_recv")
+    for c in range(per):
+        first = lrecv[:, c].astype(jnp.float32).reshape(n * rows, width).astype(jnp.bfloat16)
+        second = rrecv[:, c].astype(jnp.float32).reshape(n * rows, width).astype(jnp.bfloat16)
+        product = lax.dot_general(
+            first, second, (((1,), (1,)), ((), ())), preferred_element_type=jnp.float32
+        )
+        back[:, c] = product.reshape(n, rows, n * rows).astype(jnp.bfloat16)
+    run(home, "start")
+    out[me] = back[me]
+    run(there, "wait_send")
+    run(home, "wait_recv")
+    run(home, "wait_send")
+
+
+def triangle(left, right, n):
+    return pl.pallas_call(
+        functools.partial(triangle_kernel, n),
+        out_shape=jax.ShapeDtypeStruct(left.shape, left.dtype),
+        in_specs=[pl.BlockSpec(memory_space=pltpu.VMEM)] * 2,
+        out_specs=pl.BlockSpec(memory_space=pltpu.VMEM),
+        scratch_shapes=[pltpu.VMEM(left.shape, left.dtype)] * 3
+        + [pltpu.SemaphoreType.DMA((n,))] * 6,
+        compiler_params=pltpu.CompilerParams(collective_id=1, has_side_effects=True),
+    )(left, right)
+
+
+def per_device_direct(
+    n,
+    alignment_embedding,
+    couple_embedding,
+    tensor_first_matrix,
+    tensor_second_matrix,
+    tensor_final_matrix,
+    trimul_entry_matrix,
+    trimul_sigmoid_matrix,
+    trimul_final_matrix,
+):
+    alignment_height, rows, _ = alignment_embedding.shape
+    side = tensor_second_matrix.shape[1]
+    normal = standardize_fn(alignment_embedding.astype(jnp.float32), -1).astype(jnp.bfloat16)
+    block = jnp.einsum(
+        "ziv,vl->ilz", normal, tensor_second_matrix, preferred_element_type=jnp.float32
+    ).astype(jnp.bfloat16)
+    gathered = gather(block.reshape(rows * side, alignment_height), n)
+    right_rows = gathered.reshape(n * rows, side, alignment_height)
+    first_operand = jnp.einsum(
+        "ziv,vl->zil", normal, tensor_first_matrix, preferred_element_type=jnp.float32
+    ).astype(jnp.bfloat16)
+    outer = jnp.einsum(
+        "sic,jes->ijce", first_operand, right_rows, preferred_element_type=jnp.float32
+    )
+    outer = (outer * (1.0 / alignment_height)).astype(jnp.bfloat16)
+    outer = outer.reshape(rows, n * rows, -1)
+    update = jnp.einsum(
+        "ijf,fz->ijz", outer, tensor_final_matrix, preferred_element_type=jnp.float32
+    )
+    lifted = (couple_embedding.astype(jnp.float32) + update).astype(jnp.bfloat16)
+    normed = standardize_fn(lifted.astype(jnp.float32), -1).astype(jnp.bfloat16)
+    projected = jnp.einsum(
+        "rkz,qzc->qcrk", normed, trimul_entry_matrix, preferred_element_type=jnp.float32
+    )
+    left_t = (jax.nn.sigmoid(projected[0]) * projected[1]).astype(jnp.bfloat16)
+    right_t = (jax.nn.sigmoid(projected[2]) * projected[3]).astype(jnp.bfloat16)
+    shape = (n, left_t.shape[0] // n) + left_t.shape[1:]
+    returned = triangle(left_t.reshape(shape), right_t.reshape(shape), n)
+    summed = returned.reshape(left_t.shape)
+    tri_n = standardize_fn(summed.astype(jnp.float32), 0).astype(jnp.bfloat16)
+    out = jnp.einsum("crj,cz->rjz", tri_n, trimul_final_matrix, preferred_element_type=jnp.float32)
+    gate = jax.nn.sigmoid(
+        jnp.einsum("rjz,zy->rjy", normed, trimul_sigmoid_matrix, preferred_element_type=jnp.float32)
+    )
+    return (lifted.astype(jnp.float32) + gate * out).astype(jnp.bfloat16)
+
+
 def solution(mesh):
+    n = mesh.shape["dap"]
+    direct = mesh.shape["ch"] == 1 and n % (CORES * PLANE) == 0
+    body = functools.partial(per_device_direct, n) if direct else per_device
     placed = (
         P(None, "dap", None),
         P("dap", "ch", None),
@@ -88,5 +299,5 @@
         P(),
     )
     return jax.shard_map(
-        per_device, mesh=mesh, in_specs=placed, out_specs=P("dap", "ch", None), check_vma=False
-    )
+        body, mesh=mesh, in_specs=placed, out_specs=P("dap", "ch", None), check_vma=False
+    )

time: 115 us -> 52 us (0.45)
  waiting for transfers between devices: 79.7 us -> 0 us
  Pallas kernels: 0 us -> 37.2 us
  between operations: 13.7 us -> 0.21 us
  starting transfers between devices: 8.77 us -> 0 us
  other arithmetic: 3.28 us -> 5.24 us
    all_gather x1 -> x0, waiting for transfers between devices: 56.3 us -> none  [per_device(): right_all = lax.all_gather(second_operand, 'dap', axis=1, tiled=True)]
    pallas_call x0 -> x2, Pallas kernels: none -> 37.2 us  [the longest x1 20 us: triangle(): pl.pallas_call(functools.partial(triangle_kernel, n), out_shape=jax.Shape...]
    all_to_all x3 -> x0, waiting for transfers between devices: 23.4 us -> none  [the longest x1 8.05 us: per_device(): lax.all_to_all(left_t, 'dap', split_axis=0, concat_axis=1, tiled=True)]
    all_to_all x3 -> x0, starting transfers between devices: 8.73 us -> none  [the longest x1 3.58 us: per_device(): lax.all_to_all(right_t, 'dap', split_axis=0, concat_axis=1, tiled=True)]
    convert_element_type x6 -> x5, local copies, waits for them, and re-layouts: 3.81 us -> 3.99 us  [the longest x1 1.04 us: per_device_direct(): tri_n = standardize_fn(summed.astype(jnp.float32), 0).astype(jnp.bfloat16)]
    dot_general x7 -> x6, matrix products: 4.1 us -> 4.06 us  [the longest x1 1.9 us: per_device_direct(): jnp.einsum('sic,jes->ijce', first_operand, right_rows, preferred_element_...]
  transfers between devices with their start and end apart: 4 -> 0, of which waited for: 4 -> 0; matrix products, arithmetic and copies ran while one was open for 1% -> 0% of each run, Pallas kernels for 0% -> 0%
where the time goes in v1:
time: 52 us; the launch traced here: 51.6 us
  Pallas kernels  37.2 us (72%)
  other arithmetic  5.24 us (10%)
  local copies, waits for them, and re-layouts  4.83 us (9%)
  matrix products  4.06 us (8%)
    pallas_call x1, Pallas kernels, triangle(): pl.pallas_call(functools.partial(triangle_kernel, n), out_shape=jax.Shape...  20 us
    pallas_call x1, Pallas kernels, gather(): pl.pallas_call(functools.partial(gather_kernel, n), out_shape=jax.ShapeDt...  17.2 us
    reduce_sum x3, other arithmetic, standardize_fn(): var = jnp.mean(centred * centred, axis=axis, keepdims=True)  2.42 us
    reduce_sum x2, other arithmetic, standardize_fn(): mean = jnp.mean(value, axis=axis, keepdims=True)  2.28 us
    dot_general x1, matrix products, per_device_direct(): jnp.einsum('sic,jes->ijce', first_operand, right_rows, preferred_element_...  1.9 us
    convert_element_type x1, local copies, waits for them, and re-layouts, per_device_direct(): tri_n = standardize_fn(summed.astype(jnp.float32), 0).astype(jnp.bfloat16)  1.04 us

profile of v1, /device:TPU:0, one launch (start us, length us, event | category | flops | bytes accessed | tf_op | source)
XLA Modules:
  0.0 51.6 jit_solution(17970122459873383270)
XLA Ops:
  0.0 0.0 copy-start
  0.0 0.0 copy-start.1
  0.0 0.0 copy-start.7
  0.0 1.2 %convert_reduce_fusion = f32[128,4]{1,0:T(8,128)S(1)} fusion(bf16[128,4,256]{2,1,0:T(4,128)(2,1)} %param.8), kind=kLoop, calls=%fused_computation.18 | loop fusion | flops 261632 | bytes 264192 | tf_op jit(solution)/shard_map/reduce_sum | solution.py:15
  1.3 1.3 %fusion.12 = f32[128,4]{1,0:T(8,128)S(1)} fusion(bf16[128,4,256]{2,1,0:T(4,128)(2,1)} %param.8, f32[128,4]{1,0:T(8,128)S(1)} %broadcast_multiply_fusion), kind=kLoop, calls=%fused_computation.21 | loop fusion | flops 523776 | bytes 266240 | tf_op jit(solution)/shard_map/reduce_sum | solution.py:17
  2.6 0.0 copy-done.1
  2.6 0.0 copy-start.5
  2.6 0.3 fusion.13
  3.0 0.0 copy-done.7
  3.0 0.8 %convolution_convert_fusion.1 = bf16[128,4,32]{0,2,1:T(8,128)(2,1)} fusion(bf16[128,4,256]{2,1,0:T(4,128)(2,1)S(1)} %fusion.13, bf16[256,32]{0,1:T(8,128)(2,1)S(1)} %copy-done.7), kind=kOutput, calls=%fused_computation.14 | convolution fusion | flops 8404992 | bytes 311296 | tf_op jit(solution)/shard_map/ziv,vl->ilz/dot_general | solution.py:253
  3.8 17.2 %shard_map.82 = bf16[32,128,128]{2,1,0:T(8,128)(2,1)} custom-call(bf16[128,128]{1,0:T(8,128)(2,1)} %bitcast.51), custom_call_target="tpu_custom_call" | custom-call | tf_op jit(solution)/shard_map/pallas_call | solution.py:162
  21.0 0.0 copy-done.5
  21.0 1.9 %fusion = bf16[4,128,32,32]{1,2,0,3:T(8,128)(2,1)S(1)} fusion(bf16[128,32,128,1]{2,1,0,3:T(8,128)(2,1)} %bitcast.46, bf16[128,4,256]{2,1,0:T(4,128)(2,1)S(1)} %fusion.13, bf16[256,32]{0,1:T(8,128)(2,1)S(1)} %copy-done.5), kind=kOutput, calls=%fused_computation.1 | convolution fusion | flops 143671296 | bytes 2375680 | tf_op jit(solution)/shard_map/sic,jes->ijce/dot_general | solution.py:261
  22.9 0.0 copy-start.2
  22.9 0.7 %copy.25 = bf16[4,128,32,32]{1,3,2,0:T(8,128)(2,1)S(1)} copy(bf16[4,128,32,32]{1,2,0,3:T(8,128)(2,1)S(1)} %fusion) | data formatting | bytes 2097152 | tf_op jit(solution)/shard_map/convert_element_type | solution.py:264
  23.6 0.2 copy-done.2
  23.8 0.1 copy.22
  24.0 0.0 copy-done
  24.0 0.0 copy-start.3
  24.0 0.4 fusion.35
  24.4 0.5 copy-done.3
  24.9 0.3 convolution_bitcast_fusion
  25.2 0.1 fusion.14
  25.4 0.0 copy-start.6
  25.4 0.8 %copy.32 = bf16[1,128,4,128]{3,2,1,0:T(4,128)(2,1)} copy(bf16[1,128,4,128]{3,1,0,2:T(8,128)(2,1)S(1)} %get-tuple-element.6) | data formatting | bytes 262144 | tf_op jit(solution)/shard_map/convert_element_type | solution.py:274
  26.2 0.7 %copy.33 = bf16[1,128,4,128]{3,2,1,0:T(4,128)(2,1)} copy(bf16[1,128,4,128]{3,1,0,2:T(8,128)(2,1)S(1)} %get-tuple-element.5) | data formatting | bytes 262144 | tf_op jit(solution)/shard_map/convert_element_type | solution.py:275
  26.9 0.0 copy-start.4
  26.9 20.0 %shard_map.83 = bf16[32,4,4,128]{3,2,1,0:T(4,128)(2,1)} custom-call(bf16[32,4,4,128]{3,2,1,0:T(4,128)(2,1)} %bitcast.49, bf16[32,4,4,128]{3,2,1,0:T(4,128)(2,1)} %bitcast.50), custom_call_target="tpu_custom_call" | custom-call | tf_op jit(solution)/shard_map/pallas_call | solution.py:228
  47.0 1.1 %convert_reduce_fusion.1 = f32[4,128]{1,0:T(4,128)S(1)} fusion(bf16[32,4,4,128]{3,2,1,0:T(4,128)(2,1)} %shard_map.83), kind=kLoop, calls=%fused_computation.44 | loop fusion | flops 130560 | bytes 133120 | tf_op jit(solution)/shard_map/reduce_sum | solution.py:15
  48.0 1.1 %multiply_reduce_fusion = f32[4,128]{1,0:T(4,128)S(1)} fusion(bf16[32,4,4,128]{3,2,1,0:T(4,128)(2,1)} %shard_map.83, f32[4,128]{1,0:T(4,128)S(1)} %broadcast_multiply_fusion.1), kind=kLoop, calls=%fused_computation.37 | loop fusion | flops 261632 | bytes 135168 | tf_op jit(solution)/shard_map/reduce_sum | solution.py:17
  49.1 1.0 %copy.34 = f32[128,4,128]{0,2,1:T(8,128)S(1)} copy(bf16[128,4,128]{2,1,0:T(4,128)(2,1)} %bitcast.48) | data formatting | bytes 393216 | tf_op jit(solution)/shard_map/convert_element_type | solution.py:279
  50.1 0.0 copy-done.6
  50.1 0.3 fusion.4
  50.4 0.0 copy-done.4
  50.4 0.4 fusion.5
  50.8 0.8 %copy.36 = bf16[4,128,128]{2,1,0:T(8,128)(2,1)} copy(bf16[4,128,128]{1,2,0:T(8,128)(2,1)S(1)} %fusion.5) | data formatting | bytes 262144 | tf_op jit(solution)/shard_map/convert_element_type | solution.py:284
  (7 shorter events, 0.1 us)
Async XLA Ops:
  0.0 24.0 %copy-start = (bf16[1024,128]{1,0:T(8,128)(2,1)S(1)}, bf16[1024,128]{1,0:T(8,128)(2,1)}, u32[]{:S(2)}) copy-start(bf16[1024,128]{1,0:T(8,128)(2,1)} %param.12) | copy-start | bytes 786436
  0.0 2.6 %copy-start.1 = (bf16[128,4,256]{2,1,0:T(4,128)(2,1)S(1)}, bf16[128,4,256]{2,1,0:T(4,128)(2,1)}, u32[]{:S(2)}) copy-start(bf16[128,4,256]{2,1,0:T(4,128)(2,1)} %param.8) | copy-start | bytes 786436
  0.0 3.0 %copy-start.7 = (bf16[256,32]{0,1:T(8,128)(2,1)S(1)}, bf16[256,32]{0,1:T(8,128)(2,1)}, u32[]{:S(2)}) copy-start(bf16[256,32]{0,1:T(8,128)(2,1)} %param.11) | copy-start | bytes 49156
  2.6 18.4 %copy-start.5 = (bf16[256,32]{0,1:T(8,128)(2,1)S(1)}, bf16[256,32]{0,1:T(8,128)(2,1)}, u32[]{:S(2)}) copy-start(bf16[256,32]{0,1:T(8,128)(2,1)} %param.10) | copy-start | bytes 49156
  22.9 0.9 %copy-start.2 = (bf16[4,128,128]{2,1,0:T(8,128)(2,1)S(1)}, bf16[4,128,128]{2,1,0:T(8,128)(2,1)}, u32[]{:S(2)}) copy-start(bf16[4,128,128]{2,1,0:T(8,128)(2,1)} %param.9) | copy-start | bytes 393220
  24.0 0.9 %copy-start.3 = (bf16[4,128,128]{2,1,0:T(8,128)(2,1)S(1)}, bf16[4,128,128]{2,1,0:T(8,128)(2,1)}, u32[]{:S(2)}) copy-start(bf16[4,128,128]{2,1,0:T(8,128)(2,1)} %param.13) | copy-start | bytes 393220
  25.4 24.7 %copy-start.6 = (bf16[128,128]{1,0:T(8,128)(2,1)S(1)}, bf16[128,128]{1,0:T(8,128)(2,1)}, u32[]{:S(2)}) copy-start(bf16[128,128]{1,0:T(8,128)(2,1)} %param.14) | copy-start | bytes 98308
  26.9 23.5 %copy-start.4 = (bf16[128,128]{1,0:T(8,128)(2,1)S(1)}, bf16[128,128]{1,0:T(8,128)(2,1)}, u32[]{:S(2)}) copy-start(bf16[128,128]{1,0:T(8,128)(2,1)} %param.15) | copy-start | bytes 98308

commit v2 on v0

--- a/solution.py
+++ b/solution.py
@@ -1,7 +1,14 @@
+import functools
+
 import jax
 import jax.numpy as jnp
 from jax import lax
+from jax.experimental import pallas as pl
+from jax.experimental.pallas import tpu as pltpu
 from jax.sharding import PartitionSpec as P
+
+CORES = 2
+PLANE = 4
 
 
 def standardize_fn(value, axis):
@@ -76,7 +83,323 @@
     return (lifted.astype(jnp.float32) + gate * out).astype(jnp.bfloat16)
 
 
+def remote(src, dst, send_sem, recv_sem, peer):
+    return pltpu.make_async_remote_copy(
+        src_ref=src,
+        dst_ref=dst,
+        send_sem=send_sem,
+        recv_sem=recv_sem,
+        device_id={"dap": peer},
+        device_id_type=pl.DeviceIdType.MESH,
+    )
+
+
+def signal(peer):
+    pl.semaphore_signal(
+        pltpu.get_barrier_semaphore(),
+        inc=1,
+        device_id={"dap": peer},
+        device_id_type=pl.DeviceIdType.MESH,
+    )
+
+
+def normalized(value, axis):
+    mean = jnp.mean(value, axis=axis, keepdims=True)
+    centred = value - mean
+    var = jnp.mean(centred * centred, axis=axis, keepdims=True)
+    return centred * lax.rsqrt(var + 1e-05)
+
+
+def fused_kernel(
+    n,
+    msa,
+    first_t,
+    second_t,
+    couple_h,
+    final_h,
+    entry_h,
+    sigmoid_h,
+    output_h,
+    result,
+    couple,
+    final,
+    entry,
+    sigmoid_w,
+    output_w,
+    rows_f32,
+    final_f32,
+    block,
+    rall,
+    rmat,
+    tmat,
+    lifted_s,
+    gate_s,
+    lsend,
+    rsend,
+    lrecv,
+    rrecv,
+    back,
+    trecv,
+    local,
+    zs,
+    zr,
+    ps,
+    pr,
+    cs,
+    cr,
+    ls,
+    lr,
+    rs,
+    rr,
+    bs,
+    br,
+):
+    f32, bf16 = jnp.float32, jnp.bfloat16
+    height, rows, feat = msa.shape
+    side = first_t.shape[0]
+    width = couple.shape[2]
+    columns = couple.shape[1]
+    per = lsend.shape[1]
+    depth = n // (CORES * PLANE)
+    me = lax.axis_index("dap")
+    core, p, z = me % CORES, (me // CORES) % PLANE, me // (CORES * PLANE)
+
+    def greet(d, carry):
+        signal((me + d) % n)
+        return carry
+
+    lax.fori_loop(1, n, greet, 0)
+
+    loads = [
+        pltpu.make_async_copy(src, dst, local.at[k])
+        for k, (src, dst) in enumerate(
+            (
+                (final_h, final),
+                (couple_h, couple),
+                (entry_h, entry),
+                (sigmoid_h, sigmoid_w),
+                (output_h, output_w),
+            )
+        )
+    ]
+    for load in loads:
+        load.start()
+
+    x = msa[...].astype(f32).reshape(height * rows, feat)
+    normal = normalized(x, -1).astype(bf16)
+    weights = jnp.concatenate(
+        [first_t[...], second_t[...], jnp.zeros((128 - 2 * side, feat), bf16)], axis=0
+    )
+    rows_f32[...] = lax.dot_general(
+        normal, weights, (((1,), (1,)), ((), ())), preferred_element_type=f32
+    )
+    lefts = []
+    rights = []
+    for i in range(rows):
+        both = rows_f32[pl.ds(i, height, stride=rows), :]
+        lefts.append(both[:, :side].astype(bf16))
+        rights.append(both.T[side : 2 * side, :])
+    for i in range(rows):
+        rows_f32[pl.ds(i, side, stride=rows), :] = rights[i]
+    block[...] = rows_f32[pl.ds(0, side * rows), :].reshape(side, rows, height).astype(bf16)
+    left_all = jnp.concatenate(lefts, axis=0)
+
+    pl.semaphore_wait(pltpu.get_barrier_semaphore(), n - 1)
+
+    def device(z_, p_, core_):
+        return (z_ * PLANE + p_) * CORES + core_
+
+    def source(zi, q):
+        return device((z - zi + depth) % depth, (p - q + PLANE) % PLANE, core)
+
+    partner = me + 1 - 2 * core
+    copies = []
+
+    def send(src, slot, send_sem, recv_sem, peer):
+        copy = remote(src, rall.at[slot], send_sem, recv_sem, peer)
+        copy.start()
+        copies.append(copy)
+        return copy
+
+    along = {}
+    for zi in range(1, depth):
+        along[zi] = send(block, me, zs.at[zi], zr.at[zi], device((z + zi) % depth, p, core))
+    across = {}
+
+    def spread(zi, src):
+        slot = source(zi, 0)
+        for q in range(1, PLANE):
+            across[zi, q] = send(
+                src, slot, ps.at[zi, q], pr.at[zi, q], device(z, (p + q) % PLANE, core)
+            )
+        across[zi, 0] = send(src, slot, cs.at[zi, 0], cr.at[zi, 0], partner)
+
+    spread(0, block)
+    rall[me] = block[...]
+    loads[0].wait()
+    final_f32[...] = final[...].astype(f32)
+    for zi in range(1, depth):
+        along[zi].wait_recv()
+        spread(zi, rall.at[source(zi, 0)])
+
+    for e in range(side):
+        w_e = final_f32[pl.ds(e, side, stride=side), :].astype(bf16)
+        t_e = jnp.dot(left_all, w_e, preferred_element_type=f32).astype(bf16)
+        for i in range(rows):
+            tmat[
+                i // 2, e * height : (e + 1) * height, (i % 2) * width : (i % 2 + 1) * width
+            ] = t_e[i * height : (i + 1) * height]
+
+    over = [across[zi, 0] for zi in range(depth)]
+    for zi in range(depth):
+        for q in range(1, PLANE):
+            across[zi, q].wait_recv()
+            slot = source(zi, q)
+            over.append(send(rall.at[slot], slot, cs.at[zi, q], cr.at[zi, q], partner))
+    for load in loads[1:]:
+        load.wait()
+    for copy in over:
+        copy.wait_recv()
+
+    for e in range(side):
+        rmat[:, e * height : (e + 1) * height] = (
+            rall[:, e].astype(f32).reshape(n * rows, height).astype(bf16)
+        )
+    parts = []
+    for h in range(rows // 2):
+        update = jnp.dot(rmat[...], tmat[h], preferred_element_type=f32) * (1.0 / height)
+        for i in range(2):
+            total = couple[2 * h + i].astype(f32) + update[:, i * width : (i + 1) * width]
+            parts.append(total.astype(bf16))
+    lifted = jnp.concatenate(parts, axis=0).astype(f32)
+    lifted_s[...] = lifted
+    normed = normalized(lifted, -1).astype(bf16)
+
+    def project(q):
+        return lax.dot_general(
+            entry[q], normed, (((0,), (1,)), ((), ())), preferred_element_type=f32
+        )
+
+    def gated(q, dst):
+        value = jax.nn.sigmoid(project(q)) * project(q + 1)
+        channels = value.shape[0]
+        for i in range(rows):
+            rows_f32[pl.ds(i, channels, stride=rows), :] = value[
+                :, i * columns : (i + 1) * columns
+            ]
+        dst[...] = rows_f32[...].reshape(n, per, rows, columns).astype(bf16)
+
+    def run(make, action):
+        def step(d, carry):
+            getattr(make((me + d) % n, d), action)()
+            return carry
+
+        lax.fori_loop(1, n, step, 0)
+
+    def to_left(peer, d):
+        return remote(lsend.at[peer], lrecv.at[me], ls.at[d], lr.at[d], peer)
+
+    def to_right(peer, d):
+        return remote(rsend.at[peer], rrecv.at[me], rs.at[d], rr.at[d], peer)
+
+    def home(peer, d):
+        return remote(back.at[peer], trecv.at[me], bs.at[d], br.at[d], peer)
+
+    gated(0, lsend)
+    run(to_left, "start")
+    gated(2, rsend)
+    run(to_right, "start")
+    lrecv[me] = lsend[me]
+    rrecv[me] = rsend[me]
+    gate_s[...] = jax.nn.sigmoid(jnp.dot(normed, sigmoid_w[...], preferred_element_type=f32))
+    run(to_left, "wait_recv")
+    run(to_right, "wait_recv")
+    for c in range(per):
+        first = lrecv[:, c].astype(f32).reshape(n * rows, columns).astype(bf16)
+        second = rrecv[:, c].astype(f32).reshape(n * rows, columns).astype(bf16)
+        product = lax.dot_general(
+            first, second, (((1,), (1,)), ((), ())), preferred_element_type=f32
+        )
+        back[:, c] = product.reshape(n, rows, n * rows).astype(bf16)
+    run(home, "start")
+    trecv[me] = back[me]
+    run(to_left, "wait_send")
+    run(to_right, "wait_send")
+    for copy in copies:
+        copy.wait_send()
+    run(home, "wait_recv")
+    rows_f32[...] = trecv[...].astype(f32).reshape(n * per * rows, columns)
+    for i in range(rows):
+        tri = rows_f32[pl.ds(i, n * per, stride=rows), :]
+        tri_n = normalized(tri, 0).astype(bf16)
+        out = lax.dot_general(
+            tri_n, output_w[...], (((0,), (0,)), ((), ())), preferred_element_type=f32
+        )
+        span = slice(i * columns, (i + 1) * columns)
+        result[i] = (lifted_s[span] + gate_s[span] * out).astype(bf16)
+    run(home, "wait_send")
+
+
+def per_device_fused(
+    n,
+    alignment_embedding,
+    couple_embedding,
+    tensor_first_matrix,
+    tensor_second_matrix,
+    tensor_final_matrix,
+    trimul_entry_matrix,
+    trimul_sigmoid_matrix,
+    trimul_final_matrix,
+):
+    height, rows, _ = alignment_embedding.shape
+    side = tensor_second_matrix.shape[1]
+    columns, width = couple_embedding.shape[1:]
+    channels = trimul_entry_matrix.shape[2]
+    depth = n // (CORES * PLANE)
+    f32, bf16 = jnp.float32, jnp.bfloat16
+    wide = (n, channels // n, rows, columns)
+    late = (
+        couple_embedding,
+        tensor_final_matrix,
+        trimul_entry_matrix,
+        trimul_sigmoid_matrix,
+        trimul_final_matrix,
+    )
+    return pl.pallas_call(
+        functools.partial(fused_kernel, n),
+        out_shape=jax.ShapeDtypeStruct(couple_embedding.shape, bf16),
+        in_specs=[pl.BlockSpec(memory_space=pltpu.VMEM)] * 3
+        + [pl.BlockSpec(memory_space=pl.ANY)] * len(late),
+        out_specs=pl.BlockSpec(memory_space=pltpu.VMEM),
+        scratch_shapes=[pltpu.VMEM(a.shape, a.dtype) for a in late]
+        + [
+            pltpu.VMEM((height * rows, 128), f32),
+            pltpu.VMEM(tensor_final_matrix.shape, f32),
+            pltpu.VMEM((side, rows, height), bf16),
+            pltpu.VMEM((n, side, rows, height), bf16),
+            pltpu.VMEM((n * rows, side * height), bf16),
+            pltpu.VMEM((rows // 2, side * height, 2 * width), bf16),
+            pltpu.VMEM((rows * columns, width), f32),
+            pltpu.VMEM((rows * columns, width), f32),
+        ]
+        + [pltpu.VMEM(wide, bf16)] * 6
+        + [pltpu.SemaphoreType.DMA((len(late),))]
+        + [pltpu.SemaphoreType.DMA((depth,))] * 2
+        + [pltpu.SemaphoreType.DMA((depth, PLANE))] * 4
+        + [pltpu.SemaphoreType.DMA((n,))] * 6,
+        compiler_params=pltpu.CompilerParams(collective_id=0, has_side_effects=True),
+    )(
+        alignment_embedding,
+        tensor_first_matrix.T,
+        tensor_second_matrix.T,
+        *late,
+    )
+
+
 def solution(mesh):
+    n = mesh.shape["dap"]
+    direct = mesh.shape["ch"] == 1 and n % (CORES * PLANE) == 0
+    body = functools.partial(per_device_fused, n) if direct else per_device
     placed = (
         P(None, "dap", None),
         P("dap", "ch", None),
@@ -88,5 +411,5 @@
         P(),
     )
     return jax.shard_map(
-        per_device, mesh=mesh, in_specs=placed, out_specs=P("dap", "ch", None), check_vma=False
-    )
+        body, mesh=mesh, in_specs=placed, out_specs=P("dap", "ch", None), check_vma=False
+    )

time: 115 us -> 37.3 us (0.32)
  waiting for transfers between devices: 79.7 us -> 0 us
  Pallas kernels: 0 us -> 35.5 us
  between operations: 13.7 us -> 0.01 us
  starting transfers between devices: 8.77 us -> 0 us
  matrix products: 4.1 us -> 0 us
  other arithmetic: 3.28 us -> 0 us
  local copies, waits for them, and re-layouts: 4.68 us -> 1.57 us
    all_gather x1 -> x0, waiting for transfers between devices: 56.3 us -> none  [per_device(): right_all = lax.all_gather(second_operand, 'dap', axis=1, tiled=True)]
    pallas_call x0 -> x1, Pallas kernels: none -> 35.5 us  [per_device_fused(): pl.pallas_call(functools.partial(fused_kernel, n), out_shape=jax.ShapeDty...]
    all_to_all x3 -> x0, waiting for transfers between devices: 23.4 us -> none  [the longest x1 8.05 us: per_device(): lax.all_to_all(left_t, 'dap', split_axis=0, concat_axis=1, tiled=True)]
    all_to_all x3 -> x0, starting transfers between devices: 8.73 us -> none  [the longest x1 3.58 us: per_device(): lax.all_to_all(right_t, 'dap', split_axis=0, concat_axis=1, tiled=True)]
    dot_general x7 -> x0, matrix products: 4.1 us -> none  [the longest x1 1.9 us: outer_update(): jnp.einsum('sic,sje->ijce', first_operand, right_rows, preferred_element_...]
    convert_element_type x6 -> x0, local copies, waits for them, and re-layouts: 3.81 us -> none  [the longest x1 0.79 us: per_device(): left_t = (jax.nn.sigmoid(projected[0]) * projected[1]).astype(jnp.bfloat16)]
    reduce_sum x5 -> x0, other arithmetic: 2.73 us -> none  [the longest x3 1.46 us: standardize_fn(): var = jnp.mean(centred * centred, axis=axis, keepdims=True)]
  transfers between devices with their start and end apart: 4 -> 0, of which waited for: 4 -> 0; matrix products, arithmetic and copies ran while one was open for 1% -> 0% of each run, Pallas kernels for 0% -> 0%
where the time goes in v2:
time: 37.3 us; the launch traced here: 37.1 us
  Pallas kernels  35.5 us (95%)
  local copies, waits for them, and re-layouts  1.57 us (4%)
    pallas_call x1, Pallas kernels, per_device_fused(): pl.pallas_call(functools.partial(fused_kernel, n), out_shape=jax.ShapeDty...  35.5 us
    unnamed x1, local copies, waits for them, and re-layouts  1.57 us

profile of v2, /device:TPU:0, one launch (start us, length us, event | category | flops | bytes accessed | tf_op | source)
XLA Modules:
  0.0 37.1 jit_solution(16909495132712709906)
XLA Ops:
  0.0 35.5 %shard_map.82 = bf16[4,128,128]{2,1,0:T(8,128)(2,1)} custom-call(bf16[128,4,256]{2,1,0:T(4,128)(2,1)} %msa.1, bf16[32,256]{1,0:T(8,128)(2,1)} %bitcast.2, bf16[32,256]{1,0:T(8,128)(2,1)} %bitcast.3, bf16[4,128,128]{2,1,0:T(8,128)(2,1)} %couple_h.1, bf16[1024,128]{1,0:T(8,128)(2,1)} %final_h.1, bf16[4,128,128]{2,1,0:T(8,128)(2,1)} %entry_h.1, ...), custom_call_target="tpu_custom_call" | custom-call | tf_op jit(solution)/shard_map/pallas_call | solution.py:368
  35.5 1.6 %copy.10 = bf16[4,128,128]{2,1,0:T(8,128)(2,1)} copy(bf16[4,128,128]{2,1,0:T(8,128)(2,1)} %shard_map.82) | data formatting | bytes 262144

commit v3 on v2

--- a/solution.py
+++ b/solution.py
@@ -112,15 +112,18 @@
 
 def fused_kernel(
     n,
-    msa,
-    first_t,
-    second_t,
+    msa_h,
+    first_h,
+    second_h,
     couple_h,
     final_h,
     entry_h,
     sigmoid_h,
     output_h,
     result,
+    msa,
+    first_t,
+    second_t,
     couple,
     final,
     entry,
@@ -174,6 +177,9 @@
         pltpu.make_async_copy(src, dst, local.at[k])
         for k, (src, dst) in enumerate(
             (
+                (msa_h, msa),
+                (first_h, first_t),
+                (second_h, second_t),
                 (final_h, final),
                 (couple_h, couple),
                 (entry_h, entry),
@@ -185,12 +191,14 @@
     for load in loads:
         load.start()
 
+    for load in loads[:3]:
+        load.wait()
     x = msa[...].astype(f32).reshape(height * rows, feat)
     normal = normalized(x, -1).astype(bf16)
     weights = jnp.concatenate(
         [first_t[...], second_t[...], jnp.zeros((128 - 2 * side, feat), bf16)], axis=0
     )
-    rows_f32[...] = lax.dot_general(
+    rows_f32[pl.ds(0, height * rows), :] = lax.dot_general(
         normal, weights, (((1,), (1,)), ((), ())), preferred_element_type=f32
     )
     lefts = []
@@ -236,7 +244,7 @@
 
     spread(0, block)
     rall[me] = block[...]
-    loads[0].wait()
+    loads[3].wait()
     final_f32[...] = final[...].astype(f32)
     for zi in range(1, depth):
         along[zi].wait_recv()
@@ -256,7 +264,7 @@
             across[zi, q].wait_recv()
             slot = source(zi, q)
             over.append(send(rall.at[slot], slot, cs.at[zi, q], cr.at[zi, q], partner))
-    for load in loads[1:]:
+    for load in loads[4:]:
         load.wait()
     for copy in over:
         copy.wait_recv()
@@ -287,7 +295,8 @@
             rows_f32[pl.ds(i, channels, stride=rows), :] = value[
                 :, i * columns : (i + 1) * columns
             ]
-        dst[...] = rows_f32[...].reshape(n, per, rows, columns).astype(bf16)
+        scattered = rows_f32[pl.ds(0, channels * rows), :]
+        dst[...] = scattered.reshape(n, per, rows, columns).astype(bf16)
 
     def run(make, action):
         def step(d, carry):
@@ -328,7 +337,9 @@
     for copy in copies:
         copy.wait_send()
     run(home, "wait_recv")
-    rows_f32[...] = trecv[...].astype(f32).reshape(n * per * rows, columns)
+    rows_f32[pl.ds(0, n * per * rows), :] = (
+        trecv[...].astype(f32).reshape(n * per * rows, columns)
+    )
     for i in range(rows):
         tri = rows_f32[pl.ds(i, n * per, stride=rows), :]
         tri_n = normalized(tri, 0).astype(bf16)
@@ -358,7 +369,10 @@
     depth = n // (CORES * PLANE)
     f32, bf16 = jnp.float32, jnp.bfloat16
     wide = (n, channels // n, rows, columns)
-    late = (
+    operands = (
+        alignment_embedding,
+        tensor_first_matrix.T,
+        tensor_second_matrix.T,
         couple_embedding,
         tensor_final_matrix,
         trimul_entry_matrix,
@@ -368,12 +382,11 @@
     return pl.pallas_call(
         functools.partial(fused_kernel, n),
         out_shape=jax.ShapeDtypeStruct(couple_embedding.shape, bf16),
-        in_specs=[pl.BlockSpec(memory_space=pltpu.VMEM)] * 3
-        + [pl.BlockSpec(memory_space=pl.ANY)] * len(late),
+        in_specs=[pl.BlockSpec(memory_space=pl.ANY)] * len(operands),
         out_specs=pl.BlockSpec(memory_space=pltpu.VMEM),
-        scratch_shapes=[pltpu.VMEM(a.shape, a.dtype) for a in late]
+        scratch_shapes=[pltpu.VMEM(a.shape, a.dtype) for a in operands]
         + [
-            pltpu.VMEM((height * rows, 128), f32),
+            pltpu.VMEM((max(height, channels) * rows, 128), f32),
             pltpu.VMEM(tensor_final_matrix.shape, f32),
             pltpu.VMEM((side, rows, height), bf16),
             pltpu.VMEM((n, side, rows, height), bf16),
@@ -383,17 +396,14 @@
             pltpu.VMEM((rows * columns, width), f32),
         ]
         + [pltpu.VMEM(wide, bf16)] * 6
-        + [pltpu.SemaphoreType.DMA((len(late),))]
+        + [pltpu.SemaphoreType.DMA((len(operands),))]
         + [pltpu.SemaphoreType.DMA((depth,))] * 2
         + [pltpu.SemaphoreType.DMA((depth, PLANE))] * 4
         + [pltpu.SemaphoreType.DMA((n,))] * 6,
-        compiler_params=pltpu.CompilerParams(collective_id=0, has_side_effects=True),
-    )(
-        alignment_embedding,
-        tensor_first_matrix.T,
-        tensor_second_matrix.T,
-        *late,
-    )
+        compiler_params=pltpu.CompilerParams(
+            collective_id=0, has_side_effects=True
+        ),
+    )(*operands)
 
 
 def solution(mesh):

time: 37.3 us -> 36.4 us (0.976)
  Pallas kernels: 35.5 us -> 34.6 us
    pallas_call x1, Pallas kernels: 35.5 us -> 34.6 us  [per_device_fused(): pl.pallas_call(functools.partial(fused_kernel, n), out_shape=jax.ShapeDty...]
where the time goes in v3:
time: 36.4 us; the launch traced here: 36.2 us
  Pallas kernels  34.6 us (95%)
  local copies, waits for them, and re-layouts  1.57 us (4%)
    pallas_call x1, Pallas kernels, per_device_fused(): pl.pallas_call(functools.partial(fused_kernel, n), out_shape=jax.ShapeDty...  34.6 us
    unnamed x1, local copies, waits for them, and re-layouts  1.57 us

profile of v3, /device:TPU:0, one launch (start us, length us, event | category | flops | bytes accessed | tf_op | source)
XLA Modules:
  0.0 36.2 jit_solution(12678703659677422269)
XLA Ops:
  0.0 34.6 %shard_map.82 = bf16[4,128,128]{2,1,0:T(8,128)(2,1)} custom-call(bf16[128,4,256]{2,1,0:T(4,128)(2,1)} %msa_h.1, bf16[32,256]{1,0:T(8,128)(2,1)} %bitcast.2, bf16[32,256]{1,0:T(8,128)(2,1)} %bitcast.3, bf16[4,128,128]{2,1,0:T(8,128)(2,1)} %couple_h.1, bf16[1024,128]{1,0:T(8,128)(2,1)} %final_h.1, bf16[4,128,128]{2,1,0:T(8,128)(2,1)} %entry_h.1, ...), custom_call_target="tpu_custom_call" | custom-call | tf_op jit(solution)/shard_map/pallas_call | solution.py:382
  34.7 1.6 %copy.10 = bf16[4,128,128]{2,1,0:T(8,128)(2,1)} copy(bf16[4,128,128]{2,1,0:T(8,128)(2,1)} %shard_map.82) | data formatting | bytes 262144

commit v4 on v3

--- a/solution.py
+++ b/solution.py
@@ -120,7 +120,7 @@
     entry_h,
     sigmoid_h,
     output_h,
-    result,
+    result_h,
     msa,
     first_t,
     second_t,
@@ -143,7 +143,9 @@
     rrecv,
     back,
     trecv,
+    result,
     local,
+    stored,
     zs,
     zr,
     ps,
@@ -322,9 +324,12 @@
     rrecv[me] = rsend[me]
     gate_s[...] = jax.nn.sigmoid(jnp.dot(normed, sigmoid_w[...], preferred_element_type=f32))
     run(to_left, "wait_recv")
+    firsts = [
+        lrecv[:, c].astype(f32).reshape(n * rows, columns).astype(bf16) for c in range(per)
+    ]
     run(to_right, "wait_recv")
     for c in range(per):
-        first = lrecv[:, c].astype(f32).reshape(n * rows, columns).astype(bf16)
+        first = firsts[c]
         second = rrecv[:, c].astype(f32).reshape(n * rows, columns).astype(bf16)
         product = lax.dot_general(
             first, second, (((1,), (1,)), ((), ())), preferred_element_type=f32
@@ -340,6 +345,7 @@
     rows_f32[pl.ds(0, n * per * rows), :] = (
         trecv[...].astype(f32).reshape(n * per * rows, columns)
     )
+    stores = []
     for i in range(rows):
         tri = rows_f32[pl.ds(i, n * per, stride=rows), :]
         tri_n = normalized(tri, 0).astype(bf16)
@@ -348,7 +354,11 @@
         )
         span = slice(i * columns, (i + 1) * columns)
         result[i] = (lifted_s[span] + gate_s[span] * out).astype(bf16)
+        stores.append(pltpu.make_async_copy(result.at[i], result_h.at[i], stored.at[i]))
+        stores[-1].start()
     run(home, "wait_send")
+    for store in stores:
+        store.wait()
 
 
 def per_device_fused(
@@ -383,7 +393,7 @@
         functools.partial(fused_kernel, n),
         out_shape=jax.ShapeDtypeStruct(couple_embedding.shape, bf16),
         in_specs=[pl.BlockSpec(memory_space=pl.ANY)] * len(operands),
-        out_specs=pl.BlockSpec(memory_space=pltpu.VMEM),
+        out_specs=pl.BlockSpec(memory_space=pl.ANY),
         scratch_shapes=[pltpu.VMEM(a.shape, a.dtype) for a in operands]
         + [
             pltpu.VMEM((max(height, channels) * rows, 128), f32),
@@ -396,7 +406,9 @@
             pltpu.VMEM((rows * columns, width), f32),
         ]
         + [pltpu.VMEM(wide, bf16)] * 6
+        + [pltpu.VMEM(couple_embedding.shape, bf16)]
         + [pltpu.SemaphoreType.DMA((len(operands),))]
+        + [pltpu.SemaphoreType.DMA((rows,))]
         + [pltpu.SemaphoreType.DMA((depth,))] * 2
         + [pltpu.SemaphoreType.DMA((depth, PLANE))] * 4
         + [pltpu.SemaphoreType.DMA((n,))] * 6,

time: 36.4 us -> 36.2 us (level)
  no operation moved by 1% of the time
where the time goes in v4:
time: 36.2 us; the launch traced here: 36 us
  Pallas kernels  34.5 us (95%)
  local copies, waits for them, and re-layouts  1.57 us (4%)
    pallas_call x1, Pallas kernels, per_device_fused(): pl.pallas_call(functools.partial(fused_kernel, n), out_shape=jax.ShapeDty...  34.5 us
    unnamed x1, local copies, waits for them, and re-layouts  1.57 us

profile of v4, /device:TPU:0, one launch (start us, length us, event | category | flops | bytes accessed | tf_op | source)
XLA Modules:
  0.0 36.0 jit_solution(18383336204118730093)
XLA Ops:
  0.0 34.5 %shard_map.82 = bf16[4,128,128]{2,1,0:T(8,128)(2,1)} custom-call(bf16[128,4,256]{2,1,0:T(4,128)(2,1)} %msa_h.1, bf16[32,256]{1,0:T(8,128)(2,1)} %bitcast.2, bf16[32,256]{1,0:T(8,128)(2,1)} %bitcast.3, bf16[4,128,128]{2,1,0:T(8,128)(2,1)} %couple_h.1, bf16[1024,128]{1,0:T(8,128)(2,1)} %final_h.1, bf16[4,128,128]{2,1,0:T(8,128)(2,1)} %entry_h.1, ...), custom_call_target="tpu_custom_call" | custom-call | tf_op jit(solution)/shard_map/pallas_call | solution.py:392
  34.5 1.6 %copy.10 = bf16[4,128,128]{2,1,0:T(8,128)(2,1)} copy(bf16[4,128,128]{2,1,0:T(8,128)(2,1)} %shard_map.82) | data formatting | bytes 262144
